TPU v7x, 512 devices: a whole 4x4x16 slice. The times are simulated.
512 devices in a mesh: obs: 16 (over x, y), patch: 32 (over z, core).
Axes of the slice: x: 4, y: 4, z: 16, core: 2. Of those that a mesh axis runs over, the one named last changes fastest.
Arguments:
- green: float32 [20480, 20480], P('obs', 'patch'), may hold values from -0.0390625 to 0.0390625
- data: float32 [20480, 128], P('obs'), may hold values from -6 to 6
- neighbours: int32 [3, 20480], P(None, 'patch'), may hold values from 0 to 20479, as said below
- reg_weight: float32 [128], replicated, may hold values from 0.5 to 2
Outputs:
- slip: float32 [20480, 128], P('patch')
Inputs may be any that keep to these rules, and one draw needn't show every extreme that they name: `neighbours`: entry (k, i) is a patch within 128 of i; an entry equal to i is padding. Distance 128 is reached in every draw.
All inputs are finite; a program needn't handle non-finite values.
Results may differ from a plain program's by a relative error of at most 0.0001.
Values sent between devices are 32-bit elements; how exact they have to be, the bound alone decides.
A program may use at most 64 MiB of HBM per device.

v0:
```python
import jax
import jax.numpy as jnp
from jax import lax
from jax.sharding import Mesh
from jax.sharding import PartitionSpec as P

BAND = 128
ITERS = 3
PATCH = ("patch_0", "patch_1")
OBS = ("obs_0", "obs_1")
OBS_PATCH = ("obs_0", "obs_1", "patch_0", "patch_1")


def extended_2(shard, sides, width):
    for axis, dim in sides:
        size, length = (lax.axis_size(axis), shard.shape[dim])
        up = [(i, (i + 1) % size) for i in range(size - 1)]
        down = [(j, i) for i, j in up]
        last = lax.slice_in_dim(shard, length - width, length, axis=dim)
        first = lax.slice_in_dim(shard, 0, width, axis=dim)
        before = lax.ppermute(last, axis, up)
        after = lax.ppermute(first, axis, down)
        shard = jnp.concatenate([before, shard, after], axis=dim)
    return shard


def shifted(value, axis, steps):
    count = lax.axis_size(axis)
    first, last = (max(0, -steps), min(count, count - steps))
    return lax.ppermute(value, axis, [(source, source + steps) for source in range(first, last)])


def cut_along(shard, dim, length):
    before, after = (shard.shape[:dim], shard.shape[dim + 1 :])
    return jnp.moveaxis(shard.reshape(*before, length, -1, *after), dim, 0)


def summed_on_arrival(shard, axis, dim):
    length = lax.axis_size(axis)
    pieces = lax.all_to_all(cut_along(shard, dim, length), axis, 0, 0, tiled=True)
    return jnp.sum(pieces, axis=0)


def joined_along(pieces, dim):
    dims = list(pieces.shape[1:])
    dims[dim] *= pieces.shape[0]
    return jnp.moveaxis(pieces, 0, dim).reshape(dims)


def all_blocks(shard, axes, sequence):
    pieces = shard[None]
    for k in sequence:
        pieces = lax.all_gather(pieces, axes[k], axis=0, tiled=True)
    block = [lax.axis_size(axes[k]) for k in reversed(sequence)]
    pieces = pieces.reshape(*block, *shard.shape)
    turned = sorted(range(len(sequence)), key=lambda place: sequence[len(sequence) - 1 - place])
    return pieces.transpose(*turned, *range(len(sequence), pieces.ndim)).reshape(-1, *shard.shape)


def gather_axes(shard, axes, sequence, dim):
    return joined_along(all_blocks(shard, axes, sequence), dim)


def total_of_pieces(shard, axis):
    pieces = lax.all_gather(shard, axis)
    return pieces.sum(axis=0)


def sent_to_all(shard, axis):
    length = lax.axis_size(axis)
    return lax.all_to_all(
        jnp.broadcast_to(shard[None], (length, *shard.shape)), axis, 0, 0, tiled=True
    )


def taken_together(shard, axis):
    everything = sent_to_all(shard, axis)
    return jnp.sum(everything, axis=0)


def over_axes_2(shard, axes):
    for axis in axes:
        shard = lax.psum(shard, axis)
    return shard


def back_product(block, residual):
    return lax.dot_general(
        block,
        residual,
        (((0,), (0,)), ((), ())),
        precision=lax.Precision.HIGHEST,
        preferred_element_type=jnp.float32,
    )


def shards(green, data, neighbours, reg_weight):
    highest = lax.Precision.HIGHEST
    row_count, col_count = green.shape
    epochs = data.shape[1]
    n_patch = lax.axis_size(PATCH)
    offset = lax.axis_index(PATCH) * col_count
    local_ids = neighbours - offset + BAND
    obs_first = lax.axis_index(OBS) == 0
    share = row_count // n_patch
    residual = lax.dynamic_slice_in_dim(data, lax.axis_index(PATCH) * share, share, 0)

    def back_partial(residual):
        return back_product(green, gather_axes(residual, PATCH, (0, 1), 0))

    def gradient_of(residual):
        return total_of_pieces(back_partial(residual), OBS)

    def squared_norm(gradient):
        return taken_together(jnp.sum(gradient * gradient, axis=0), PATCH)

    slip = jnp.zeros((col_count, epochs), jnp.float32)
    reg_resid = jnp.zeros((col_count, epochs), jnp.float32)
    gradient = gradient_of(residual)
    grad_norm = squared_norm(gradient)
    direction = gradient
    for iteration in range(ITERS):
        image = summed_on_arrival(
            jnp.dot(green, direction, precision=highest, preferred_element_type=jnp.float32),
            PATCH,
            0,
        )
        image, image_sq = (image, jnp.sum(image * image, axis=0))
        extended = extended_2(direction, ((PATCH, 0),), BAND)
        reg_image = reg_weight * (
            4.0 * direction
            - extended[local_ids[0]]
            - extended[local_ids[1]]
            - extended[local_ids[2]]
        )
        reg_sq = jnp.where(obs_first, jnp.sum(reg_image * reg_image, axis=0), 0.0)
        curvature = over_axes_2(image_sq + reg_sq, OBS_PATCH)
        step_size = grad_norm / curvature
        slip = slip + step_size * direction
        if iteration + 1 < ITERS:
            residual = residual - step_size * image
            reg_resid = reg_resid - step_size * reg_image
            spread = jnp.zeros((col_count + 2 * BAND, epochs), jnp.float32)
            for slot in range(3):
                spread = spread.at[local_ids[slot]].add(reg_resid)
            from_left = shifted(spread[BAND + col_count :], PATCH, 1)
            from_right = shifted(spread[:BAND], PATCH, -1)
            filler = jnp.zeros((col_count - BAND, epochs), jnp.float32)
            inside = (
                spread[BAND : BAND + col_count]
                + jnp.concatenate([from_left, filler], 0)
                + jnp.concatenate([filler, from_right], 0)
            )
            gradient = gradient_of(residual) + reg_weight * (4.0 * reg_resid - inside)
            next_norm = squared_norm(gradient)
            direction = gradient + next_norm / grad_norm * direction
            grad_norm = next_norm
    return slip


def solution(mesh):
    split = Mesh(mesh.devices.reshape(4, 4, 16, 2), ("obs_0", "obs_1", "patch_0", "patch_1"))
    in_specs = (P(OBS, PATCH), P(OBS, None), P(None, PATCH), P())
    out_specs = P(PATCH, None)
    return jax.shard_map(
        shards, mesh=split, in_specs=in_specs, out_specs=out_specs, check_vma=False
    )
```

profile of v0, /device:TPU:1, one launch (start us, length us, event | category | flops | bytes accessed | tf_op | source)
XLA Modules:
  0.0 751.5 jit_solution(1936652341242088612)
XLA Ops:
  7.4 30.9 %all-gather = f32[640,128]{1,0:T(8,128)S(1)} all-gather(f32[40,128]{1,0:T(8,128)S(1)} %constant_dynamic-slice_fusion), channel_id=2, replica_groups=mesh['obs_0'=4,'obs_1'=4,'patch_0'=16,'patch_1'=2] {'patch_0'}, dimensions={0}, use_global_device_ids=true | all-gather | bytes 348160 | tf_op jit(solution)/shard_map/all_gather | solution.py:53
  38.3 9.9 %all_gather.37 = f32[32,40,128]{2,1,0:T(8,128)S(1)} all-gather(f32[16,40,128]{2,1,0:T(8,128)S(1)} %bitcast.84), channel_id=1, replica_groups=mesh['obs_0'=4,'obs_1'=4,'patch_0'=16,'patch_1'=2] {'patch_1'}, dimensions={0}, use_global_device_ids=true | all-gather | bytes 983040 | tf_op jit(solution)/shard_map/all_gather | solution.py:53
  51.3 67.2 %all-gather.10.cloned.1.call-done = f32[10240,128]{0,1:T(8,128)} async-done(((f32[640,128]{0,1:T(8,128)}), f32[10240,128]{0,1:T(8,128)}) %all-gather.10.cloned.1.call-update) | async-done | bytes 5242896 | tf_op jit(solution)/shard_map/all_gather | solution.py:65
  124.1 13.2 %all-to-all-start = ((f32[32,1,128]{2,1,0:T(1,128)}), f32[32,1,128]{2,1,0:T(1,128)S(1)}, u32[]{:S(2)}, u32[]{:S(2)}) async-start(f32[32,1,128]{2,1,0:T(1,128)} %broadcast_in_dim.21), calls=%async_computation | async-start | bytes 32768 | tf_op jit(solution)/shard_map/all_to_all | solution.py:71
  166.0 16.8 %collective-permute-done = f32[128,128]{1,0:T(8,128)S(1)} collective-permute-done((f32[128,128]{1,0:T(8,128)}, f32[128,128]{1,0:T(8,128)S(1)}, u32[]{:S(2)}, u32[]{:S(2)}) %collective-permute-start) | collective-permute-done | bytes 65568 | tf_op jit(solution)/shard_map/ppermute | solution.py:21
  202.1 8.4 %psum.84 = f32[128]{0:T(128)S(1)} all-reduce(f32[128]{0:T(128)S(1)} %fusion.23), channel_id=1, replica_groups=mesh['obs_0'=4,'obs_1'=4,'patch_0'=16,'patch_1'=2] {'obs_0'}, use_global_device_ids=true, to_apply=%region_6.7 | all-reduce | flops 128 | bytes 1024 | tf_op jit(solution)/shard_map/psum | solution.py:83
  217.0 24.1 %psum.86 = f32[128]{0:T(128)S(1)} all-reduce(f32[128]{0:T(128)S(1)} %psum.85), channel_id=1, replica_groups=mesh['obs_0'=4,'obs_1'=4,'patch_0'=16,'patch_1'=2] {'patch_0'}, use_global_device_ids=true, to_apply=%region_8.9 | all-reduce | flops 128 | bytes 1024 | tf_op jit(solution)/shard_map/psum | solution.py:83
  241.2 13.6 %psum.87 = f32[128]{0:T(128)S(1)} all-reduce(f32[128]{0:T(128)S(1)} %psum.86), channel_id=1, replica_groups=mesh['obs_0'=4,'obs_1'=4,'patch_0'=16,'patch_1'=2] {'patch_1'}, use_global_device_ids=true, to_apply=%region_9.10 | all-reduce | flops 128 | bytes 1024 | tf_op jit(solution)/shard_map/psum | solution.py:83
  255.5 21.6 %all-gather.2 = f32[640,128]{1,0:T(8,128)S(1)} all-gather(f32[40,128]{1,0:T(8,128)S(1)} %multiply_subtract_fusion.6), channel_id=4, replica_groups=mesh['obs_0'=4,'obs_1'=4,'patch_0'=16,'patch_1'=2] {'patch_0'}, dimensions={0}, use_global_device_ids=true | all-gather | bytes 348160 | tf_op jit(solution)/shard_map/all_gather | solution.py:53
  277.1 9.2 %all_gather.41 = f32[32,40,128]{2,1,0:T(8,128)S(1)} all-gather(f32[16,40,128]{2,1,0:T(8,128)S(1)} %bitcast.86), channel_id=1, replica_groups=mesh['obs_0'=4,'obs_1'=4,'patch_0'=16,'patch_1'=2] {'patch_1'}, dimensions={0}, use_global_device_ids=true | all-gather | bytes 983040 | tf_op jit(solution)/shard_map/all_gather | solution.py:53
  319.1 35.6 %all-gather.12.cloned.1.call-done = f32[10240,128]{0,1:T(8,128)} async-done(((f32[640,128]{0,1:T(8,128)}), f32[10240,128]{0,1:T(8,128)}) %all-gather.12.cloned.1.call-update) | async-done | bytes 5242896 | tf_op jit(solution)/shard_map/all_gather | solution.py:65
  363.5 24.8 %all_to_all.33 = f32[32,1,128]{2,1,0:T(1,128)S(1)} all-to-all(f32[32,1,128]{2,1,0:T(1,128)S(1)} %broadcast_in_dim.25), channel_id=1, replica_groups=mesh['obs_0'=4,'obs_1'=4,'patch_0'=16,'patch_1'=2] {'patch_0','patch_1'}, dimensions={0} | all-to-all | bytes 32768 | tf_op jit(solution)/shard_map/all_to_all | solution.py:71
  408.2 19.1 %collective-permute-done.4 = f32[128,128]{1,0:T(8,128)S(1)} collective-permute-done((f32[128,128]{1,0:T(8,128)S(1)}, f32[128,128]{1,0:T(8,128)S(1)}, u32[]{:S(2)}, u32[]{:S(2)}) %collective-permute-start.4) | collective-permute-done | bytes 65568 | tf_op jit(solution)/shard_map/ppermute | solution.py:21
  447.1 8.4 %psum.88 = f32[128]{0:T(128)S(1)} all-reduce(f32[128]{0:T(128)S(1)} %fusion.24), channel_id=1, replica_groups=mesh['obs_0'=4,'obs_1'=4,'patch_0'=16,'patch_1'=2] {'obs_0'}, use_global_device_ids=true, to_apply=%region_19.20 | all-reduce | flops 128 | bytes 1024 | tf_op jit(solution)/shard_map/psum | solution.py:83
  462.1 23.9 %psum.90 = f32[128]{0:T(128)S(1)} all-reduce(f32[128]{0:T(128)S(1)} %psum.89), channel_id=1, replica_groups=mesh['obs_0'=4,'obs_1'=4,'patch_0'=16,'patch_1'=2] {'patch_0'}, use_global_device_ids=true, to_apply=%region_21.22 | all-reduce | flops 128 | bytes 1024 | tf_op jit(solution)/shard_map/psum | solution.py:83
  486.0 13.6 %psum.91 = f32[128]{0:T(128)S(1)} all-reduce(f32[128]{0:T(128)S(1)} %psum.90), channel_id=1, replica_groups=mesh['obs_0'=4,'obs_1'=4,'patch_0'=16,'patch_1'=2] {'patch_1'}, use_global_device_ids=true, to_apply=%region_22.23 | all-reduce | flops 128 | bytes 1024 | tf_op jit(solution)/shard_map/psum | solution.py:83
  499.5 21.6 %all-gather.4 = f32[640,128]{1,0:T(8,128)S(1)} all-gather(f32[40,128]{1,0:T(8,128)S(1)} %multiply_subtract_fusion.5), channel_id=6, replica_groups=mesh['obs_0'=4,'obs_1'=4,'patch_0'=16,'patch_1'=2] {'patch_0'}, dimensions={0}, use_global_device_ids=true | all-gather | bytes 348160 | tf_op jit(solution)/shard_map/all_gather | solution.py:53
  521.1 9.2 %all_gather.45 = f32[32,40,128]{2,1,0:T(8,128)S(1)} all-gather(f32[16,40,128]{2,1,0:T(8,128)S(1)} %bitcast.85), channel_id=1, replica_groups=mesh['obs_0'=4,'obs_1'=4,'patch_0'=16,'patch_1'=2] {'patch_1'}, dimensions={0}, use_global_device_ids=true | all-gather | bytes 983040 | tf_op jit(solution)/shard_map/all_gather | solution.py:53
  564.7 34.0 %all-gather.14.cloned.1.call-done = f32[10240,128]{0,1:T(8,128)} async-done(((f32[640,128]{0,1:T(8,128)}), f32[10240,128]{0,1:T(8,128)}) %all-gather.14.cloned.1.call-update) | async-done | bytes 5242896 | tf_op jit(solution)/shard_map/all_gather | solution.py:65
  607.5 24.8 %all_to_all.34 = f32[32,1,128]{2,1,0:T(1,128)S(1)} all-to-all(f32[32,1,128]{2,1,0:T(1,128)S(1)} %broadcast_in_dim.27), channel_id=1, replica_groups=mesh['obs_0'=4,'obs_1'=4,'patch_0'=16,'patch_1'=2] {'patch_0','patch_1'}, dimensions={0} | all-to-all | bytes 32768 | tf_op jit(solution)/shard_map/all_to_all | solution.py:71
  652.2 19.2 %collective-permute-done.8 = f32[128,128]{1,0:T(8,128)S(1)} collective-permute-done((f32[128,128]{1,0:T(8,128)S(1)}, f32[128,128]{1,0:T(8,128)S(1)}, u32[]{:S(2)}, u32[]{:S(2)}) %collective-permute-start.8) | collective-permute-done | bytes 65568 | tf_op jit(solution)/shard_map/ppermute | solution.py:21
  690.4 8.4 %psum.92 = f32[128]{0:T(128)S(1)} all-reduce(f32[128]{0:T(128)S(1)} %fusion.25), channel_id=1, replica_groups=mesh['obs_0'=4,'obs_1'=4,'patch_0'=16,'patch_1'=2] {'obs_0'}, use_global_device_ids=true, to_apply=%region_32.33 | all-reduce | flops 128 | bytes 1024 | tf_op jit(solution)/shard_map/psum | solution.py:83
  705.6 23.7 %psum.94 = f32[128]{0:T(128)S(1)} all-reduce(f32[128]{0:T(128)S(1)} %psum.93), channel_id=1, replica_groups=mesh['obs_0'=4,'obs_1'=4,'patch_0'=16,'patch_1'=2] {'patch_0'}, use_global_device_ids=true, to_apply=%region_34.35 | all-reduce | flops 128 | bytes 1024 | tf_op jit(solution)/shard_map/psum | solution.py:83
  729.3 13.6 %psum.95 = f32[128]{0:T(128)S(1)} all-reduce(f32[128]{0:T(128)S(1)} %psum.94), channel_id=1, replica_groups=mesh['obs_0'=4,'obs_1'=4,'patch_0'=16,'patch_1'=2] {'patch_1'}, use_global_device_ids=true, to_apply=%region_35.36 | all-reduce | flops 128 | bytes 1024 | tf_op jit(solution)/shard_map/psum | solution.py:83
  (126 shorter events, 243.4 us)
Async XLA Ops:
  6.5 41.7 %copy-start = (f32[1280,640]{1,0:T(8,128)S(1)}, f32[1280,640]{1,0:T(8,128)}, u32[]{:S(2)}) copy-start(f32[1280,640]{1,0:T(8,128)} %param.4) | copy-start | bytes 9830404
  6.5 111.9 %all-gather.10.cloned.1.call-start = ((), (), s32[]{:S(2)}) async-start(), calls=%async_computation.6 | async-start | bytes 5570560 | tf_op jit(solution)/shard_map/all_gather | solution.py:65
  122.7 0.7 copy-start.3
  124.1 24.9 %all-to-all-start = ((f32[32,1,128]{2,1,0:T(1,128)}), f32[32,1,128]{2,1,0:T(1,128)S(1)}, u32[]{:S(2)}, u32[]{:S(2)}) async-start(f32[32,1,128]{2,1,0:T(1,128)} %broadcast_in_dim.21), calls=%async_computation | async-start | bytes 32768 | tf_op jit(solution)/shard_map/all_to_all | solution.py:71
  137.3 19.7 %copy-start.5 = (s32[3,640]{1,0:T(4,128)S(1)}, s32[3,640]{1,0:T(4,128)}, u32[]{:S(2)}) copy-start(s32[3,640]{1,0:T(4,128)} %param.6) | copy-start | bytes 23044
  149.1 51.8 %all-to-all-start.1 = ((f32[32,40,128]{2,1,0:T(8,128)}), f32[32,40,128]{2,1,0:T(8,128)}, u32[]{:S(2)}, u32[]{:S(2)}) async-start(f32[32,40,128]{2,1,0:T(8,128)} %bitcast.75), calls=%async_computation.1 | async-start | bytes 1310720 | tf_op jit(solution)/shard_map/all_to_all | solution.py:40
  157.0 197.7 %all-gather.12.cloned.1.call-start = ((), (), s32[]{:S(2)}) async-start(), calls=%async_computation.7 | async-start | bytes 5570560 | tf_op jit(solution)/shard_map/all_gather | solution.py:65
  160.5 22.3 %collective-permute-start = (f32[128,128]{1,0:T(8,128)}, f32[128,128]{1,0:T(8,128)S(1)}, u32[]{:S(2)}, u32[]{:S(2)}) collective-permute-start(f32[128,128]{1,0:T(8,128)} %get-tuple-element.24), channel_id=1, source_target_pairs={{0,1},{1,2},{2,3},{3,4},{4,5},{5,6},{6,7},{7,8},{8,9},{9,10},{10,1... | collective-permute-start | bytes 196616 | tf_op jit(solution)/shard_map/ppermute | solution.py:21
  164.1 23.2 %collective-permute-start.1 = (f32[128,128]{1,0:T(8,128)S(1)}, f32[128,128]{1,0:T(8,128)S(1)}, u32[]{:S(2)}, u32[]{:S(2)}) collective-permute-start(f32[128,128]{1,0:T(8,128)S(1)} %get-tuple-element.25), channel_id=1, source_target_pairs={{1,0},{2,1},{3,2},{4,3},{5,4},{6,5},{7,6},{8,7},{9,8},{10,9},{11,1... | collective-permute-start | bytes 196616 | tf_op jit(solution)/shard_map/ppermute | solution.py:22
  192.3 6.5 copy-start.4
  313.5 48.0 %collective-permute-start.2 = (f32[128,128]{1,0:T(8,128)}, f32[128,128]{1,0:T(8,128)S(1)}, u32[]{:S(2)}, u32[]{:S(2)}) collective-permute-start(f32[128,128]{1,0:T(8,128)} %get-tuple-element.18), channel_id=1, source_target_pairs={{0,1},{1,2},{2,3},{3,4},{4,5},{5,6},{6,7},{7,8},{8,9},{9,10},{10,1... | collective-permute-start | bytes 196616 | tf_op jit(solution)/shard_map/ppermute | solution.py:30
  316.8 44.7 %collective-permute-start.3 = (f32[128,128]{1,0:T(8,128)S(1)}, f32[128,128]{1,0:T(8,128)S(1)}, u32[]{:S(2)}, u32[]{:S(2)}) collective-permute-start(f32[128,128]{1,0:T(8,128)S(1)} %get-tuple-element.19), channel_id=1, source_target_pairs={{1,0},{2,1},{3,2},{4,3},{5,4},{6,5},{7,6},{8,7},{9,8},{10,9},{11,1... | collective-permute-start | bytes 196616 | tf_op jit(solution)/shard_map/ppermute | solution.py:30
  389.5 0.7 copy-start.1
  396.7 49.3 %all-to-all-start.3 = ((f32[32,40,128]{2,1,0:T(8,128)}), f32[32,40,128]{2,1,0:T(8,128)}, u32[]{:S(2)}, u32[]{:S(2)}) async-start(f32[32,40,128]{2,1,0:T(8,128)} %bitcast.76), calls=%async_computation.3 | async-start | bytes 1310720 | tf_op jit(solution)/shard_map/all_to_all | solution.py:40
  401.8 196.9 %all-gather.14.cloned.1.call-start = ((), (), s32[]{:S(2)}) async-start(), calls=%async_computation.8 | async-start | bytes 5570560 | tf_op jit(solution)/shard_map/all_gather | solution.py:65
  402.7 24.6 %collective-permute-start.4 = (f32[128,128]{1,0:T(8,128)S(1)}, f32[128,128]{1,0:T(8,128)S(1)}, u32[]{:S(2)}, u32[]{:S(2)}) collective-permute-start(f32[128,128]{1,0:T(8,128)S(1)} %get-tuple-element.22), channel_id=1, source_target_pairs={{0,1},{1,2},{2,3},{3,4},{4,5},{5,6},{6,7},{7,8},{8,9},{9,10},{10,1... | collective-permute-start | bytes 196616 | tf_op jit(solution)/shard_map/ppermute | solution.py:21
  406.3 26.0 %collective-permute-start.5 = (f32[128,128]{1,0:T(8,128)S(1)}, f32[128,128]{1,0:T(8,128)S(1)}, u32[]{:S(2)}, u32[]{:S(2)}) collective-permute-start(f32[128,128]{1,0:T(8,128)S(1)} %get-tuple-element.23), channel_id=1, source_target_pairs={{1,0},{2,1},{3,2},{4,3},{5,4},{6,5},{7,6},{8,7},{9,8},{10,9},{11,1... | collective-permute-start | bytes 196616 | tf_op jit(solution)/shard_map/ppermute | solution.py:22
  559.2 46.3 %collective-permute-start.6 = (f32[128,128]{1,0:T(8,128)}, f32[128,128]{1,0:T(8,128)S(1)}, u32[]{:S(2)}, u32[]{:S(2)}) collective-permute-start(f32[128,128]{1,0:T(8,128)} %get-tuple-element.16), channel_id=1, source_target_pairs={{0,1},{1,2},{2,3},{3,4},{4,5},{5,6},{6,7},{7,8},{8,9},{9,10},{10,1... | collective-permute-start | bytes 196616 | tf_op jit(solution)/shard_map/ppermute | solution.py:30
  562.5 43.0 %collective-permute-start.7 = (f32[128,128]{1,0:T(8,128)S(1)}, f32[128,128]{1,0:T(8,128)S(1)}, u32[]{:S(2)}, u32[]{:S(2)}) collective-permute-start(f32[128,128]{1,0:T(8,128)S(1)} %get-tuple-element.17), channel_id=1, source_target_pairs={{1,0},{2,1},{3,2},{4,3},{5,4},{6,5},{7,6},{8,7},{9,8},{10,9},{11,1... | collective-permute-start | bytes 196616 | tf_op jit(solution)/shard_map/ppermute | solution.py:30
  633.5 0.7 copy-start.2
  640.7 48.6 %all-to-all-start.5 = ((f32[32,40,128]{2,1,0:T(8,128)}), f32[32,40,128]{2,1,0:T(8,128)}, u32[]{:S(2)}, u32[]{:S(2)}) async-start(f32[32,40,128]{2,1,0:T(8,128)} %bitcast.77), calls=%async_computation.5 | async-start | bytes 1310720 | tf_op jit(solution)/shard_map/all_to_all | solution.py:40
  646.7 24.7 %collective-permute-start.8 = (f32[128,128]{1,0:T(8,128)S(1)}, f32[128,128]{1,0:T(8,128)S(1)}, u32[]{:S(2)}, u32[]{:S(2)}) collective-permute-start(f32[128,128]{1,0:T(8,128)S(1)} %get-tuple-element.20), channel_id=1, source_target_pairs={{0,1},{1,2},{2,3},{3,4},{4,5},{5,6},{6,7},{7,8},{8,9},{9,10},{10,1... | collective-permute-start | bytes 196616 | tf_op jit(solution)/shard_map/ppermute | solution.py:21
  650.2 26.1 %collective-permute-start.9 = (f32[128,128]{1,0:T(8,128)S(1)}, f32[128,128]{1,0:T(8,128)S(1)}, u32[]{:S(2)}, u32[]{:S(2)}) collective-permute-start(f32[128,128]{1,0:T(8,128)S(1)} %get-tuple-element.21), channel_id=1, source_target_pairs={{1,0},{2,1},{3,2},{4,3},{5,4},{6,5},{7,6},{8,7},{9,8},{10,9},{11,1... | collective-permute-start | bytes 196616 | tf_op jit(solution)/shard_map/ppermute | solution.py:22
Sparse Core Ops, SparseCore 0:
  51.4 66.9 all-gather.9
  289.5 65.0 all-gather.11
  533.5 65.1 all-gather.13
where the time goes:
time: 762 us; the launch traced here: 752 us
  blocking collectives  309 us (41%)
  waiting for transfers between devices  211 us (28%)
  other arithmetic  74.5 us (10%)
  local copies, waits for them, and re-layouts  61.7 us (8%)
  starting transfers between devices  58.8 us (8%)
  matrix products  22.9 us (3%)
  between operations  13.6 us (2%)
    psum x12, blocking collectives, over_axes_2(): shard = lax.psum(shard, axis)  157 us
    all_gather x3, waiting for transfers between devices, total_of_pieces(): pieces = lax.all_gather(shard, axis)  137 us
    all_gather x6, blocking collectives, all_blocks(): pieces = lax.all_gather(pieces, axes[k], axis=0, tiled=True)  102 us
    ppermute x3, waiting for transfers between devices, extended_2(): before = lax.ppermute(last, axis, up)  55.1 us
    all_to_all x2, blocking collectives, sent_to_all(): lax.all_to_all(jnp.broadcast_to(shard[None], (length, *shard.shape)), axi...  49.6 us
    scatter-add x6, other arithmetic, shards(): spread = spread.at[local_ids[slot]].add(reg_resid)  45 us
    all_to_all x3, starting transfers between devices, summed_on_arrival(): lax.all_to_all(cut_along(shard, dim, length), axis, 0, 0, tiled=True)  18.1 us
  transfers between devices with their start and end apart: 17, of which 10 were waited for; matrix products, arithmetic and copies ran while one was open for 15% of the time, Pallas kernels for 0%

commit v1 on v0

v1 whole, which is shorter than its diff:
```python
import jax
import jax.numpy as jnp
from jax import lax
from jax.experimental import pallas as pl
from jax.experimental.pallas import tpu as pltpu
from jax.sharding import Mesh
from jax.sharding import PartitionSpec as P

ITERS = 3
NX, NY, NZ = 4, 4, 16
XY = NX * NY
OBS = ("x", "y")
PATCH = ("z", "c")
F32, BF16 = jnp.float32, jnp.bfloat16
MESH = pl.DeviceIdType.MESH

R = 40
HALO = 7
KWIN = 384
JWIN = 640
OFFH = 256

SEMS = (
    ["g0", "g1", "g2", "g3", "g4", "data", "s_off", "r_offl", "r_offr", "s_xy", "r_xy", "s_xs", "r_xs", "s_xg", "r_xg"]
    + ["s_pa", "r_pa", "s_pair", "r_pair", "s_rs", "r_relp", "r_relm", "r_dir", "r_fin", "s_sa", "r_sa"]
    + ["s_hl", "s_hr", "r_hl", "r_hr", "s_ag", "r_aga", "r_agb", "r_ag6", "r_ag7", "s_pb", "r_pb", "s_sb", "r_sb"]
    + ["s_pag", "r_pag"]
)
SEM = {name: place for place, name in enumerate(SEMS)}


def split(value):
    high = value.astype(BF16)
    low = (value - high.astype(F32)).astype(BF16)
    return high, low


def halves(value):
    return jnp.concatenate(split(value), axis=-1)


def folded(value):
    return value[:, :128] + value[:, 128:]


def dot(a, b):
    return jnp.dot(a, b, preferred_element_type=F32)


def kernel(
    green, data, neighbours, weight, out,
    gf, ghi, glo, thi, tlo, g2, im2, part, pairb, relp, relm, dirb, fin, img, q, xyr, gext, d,
    imgown, ldown, rown, offl, lx, lxt, sca, scb, xs, pab, snd, vals, sems,
):
    x, y, z, c = (lax.axis_index(a) for a in ("x", "y", "z", "c"))
    j = x * NY + y
    sign = 1 - 2 * c
    partner = (x, y, z, 1 - c)

    def ring(step):
        return lax.rem(z + sign * step + 2 * NZ, NZ)

    def along(step):
        return (x, y, ring(step), c)

    def wrapped(place):
        return lax.rem(place + NZ, NZ)

    before = (x, y, wrapped(z - 1 + c), 1 - c)
    after = (x, y, wrapped(z + c), 1 - c)

    def plane():
        for dx in range(NX):
            for dy in range(NY):
                if dx or dy:
                    px, py = lax.rem(x + dx, NX), lax.rem(y + dy, NY)
                    yield px * NY + py, (px, py, z, c)

    def copy(src, dst, s, r, to):
        return pltpu.make_async_remote_copy(
            src_ref=src, dst_ref=dst, send_sem=sems.at[SEM[s]], recv_sem=sems.at[SEM[r]],
            device_id=to, device_id_type=MESH,
        )

    def put(src, dst, s, r, to):
        copy(src, dst, s, r, to).start()

    def got(ref, r):
        copy(ref, ref, "s_xy", r, partner).wait_recv()

    def sent(ref, s):
        copy(ref, ref, s, "r_xy", partner).wait_send()

    loads = [
        pltpu.make_async_copy(green.at[pl.ds(256 * i, 256)], gf.at[pl.ds(256 * i, 256)], sems.at[SEM["g0"] + i])
        for i in range(5)
    ]
    load_data = pltpu.make_async_copy(data, img, sems.at[SEM["data"]])
    for load in loads:
        load.start()
    load_data.start()

    cols = neighbours.shape[1]
    base = (2 * z + c) * cols
    ids = base + lax.broadcasted_iota(jnp.int32, neighbours.shape, 1)
    offl[...] = jnp.zeros_like(offl)
    offl[0:3, OFFH : OFFH + cols] = (neighbours[...] - ids).astype(F32)
    for ref in (gext, d, imgown, ldown, rown, sca, scb, xs, vals):
        ref[...] = jnp.zeros_like(ref)
    out[...] = jnp.zeros_like(out)
    vals[1:2] = jnp.ones((1, 1, 128), F32)

    barrier = pltpu.get_barrier_semaphore()
    greeted = [along(k) for k in range(1, NZ)] + [to for _, to in plane()]
    greeted += [partner, (x, y, wrapped(z - 1 + 2 * c), 1 - c)]
    for to in greeted:
        pl.semaphore_signal(barrier, inc=1, device_id=to, device_id_type=MESH)

    for i in range(5):
        loads[i].wait()
        for k in range(2):
            rows = pl.ds(256 * i + 128 * k, 128)
            block = gf[rows, :]
            ghi[rows, :], glo[rows, :] = split(block)
            thi[:, rows], tlo[:, rows] = split(block.T)
    load_data.wait()

    pl.semaphore_wait(barrier, len(greeted))
    put(offl.at[:, pl.ds(cols, OFFH)], offl.at[:, pl.ds(0, OFFH)], "s_off", "r_offl", after)
    put(offl.at[:, pl.ds(OFFH, OFFH)], offl.at[:, pl.ds(OFFH + cols, OFFH)], "s_off", "r_offr", before)

    def forward(half):
        def tile(i, _):
            rows = pl.ds(pl.multiple_of(half * 640 + i * 160, 160), 160)
            both = dot(ghi[rows, :], g2[...]) + dot(glo[rows, :], g2[...])
            part[half, pl.ds(4 * i, 4)] = folded(both).reshape(4, R, 128)
            return 0

        lax.fori_loop(0, 4, tile, 0)

    def back(half, add):
        def convert(i, _):
            rows = pl.ds(pl.multiple_of(i * 160, 160), 160)
            im2[rows, :] = halves(img[half, pl.ds(4 * i, 4)].reshape(160, 128))
            return 0

        lax.fori_loop(0, 4, convert, 0)
        depth = pl.ds(pl.multiple_of(half * 640, 128), 640)

        def tile(i, _):
            rows = pl.ds(pl.multiple_of(i * 160, 160), 160)
            both = dot(thi[rows, depth], im2[...]) + dot(tlo[rows, depth], im2[...])
            value = folded(both).reshape(4, R, 128)
            place = pl.ds(4 * i, 4)
            q[place] = q[place] + value if add else value
            return 0

        lax.fori_loop(0, 4, tile, 0)

    def exchange_curvature():
        xs[pl.ds(j, 1)] = jnp.sum(scb[...], axis=0, keepdims=True)
        for _, to in plane():
            put(xs.at[j], xs.at[j], "s_xs", "r_xs", to)

    def curvature():
        got(xs.at[pl.ds(0, XY - 1)], "r_xs")
        return jnp.sum(xs[...], axis=0)

    def step_on(scale):
        def add(i, _):
            out[i] = out[i] + scale * d[i]
            return 0

        lax.fori_loop(0, XY, add, 0)

    def build_l():
        got(offl.at[:, pl.ds(0, OFFH)], "r_offl")
        got(offl.at[:, pl.ds(0, OFFH)], "r_offr")
        pick = (
            lax.broadcasted_iota(jnp.int32, (8, 128), 0) == lax.broadcasted_iota(jnp.int32, (8, 128), 1)
        ).astype(F32)
        turned = lax.dot_general(
            offl[...].astype(BF16), pick.astype(BF16), (((0,), (0,)), ((), ())), preferred_element_type=F32
        )
        gf[0:1152, 0:128] = turned
        first = base + R * j - 160
        column = lax.broadcasted_iota(jnp.int32, (16, JWIN), 1).astype(F32)

        def rows16(i, _):
            shift = gf[pl.ds(pl.multiple_of(96 + R * j + 16 * i, 8), 16), 0:128]
            row = 16 * i + lax.broadcasted_iota(jnp.int32, (16, 1), 0)
            place = (row + 120).astype(F32)
            value = jnp.where(column == place, 4.0, 0.0)
            for slot in range(3):
                value = value - jnp.where(column == place + shift[:, slot : slot + 1], 1.0, 0.0)
            known = jnp.logical_and(first + row >= 0, first + row < cols * 2 * NZ)
            value = value * known.astype(F32)
            lx[pl.ds(pl.multiple_of(16 * i, 16), 16), :] = value.astype(BF16)
            return 0

        lax.fori_loop(0, KWIN // 16, rows16, 0)
        lxt[...] = lx[:, 256:384].astype(F32).T.astype(BF16)

    def body(it, _):
        back(c, False)

        @pl.when(it > 0)
        def _():
            got(img.at[0], "r_pag")

        back(1 - c, True)

        @pl.when(it > 0)
        def _():
            sent(img.at[0], "s_pag")
            got(scb.at[pl.ds(0, NZ - 1)], "r_sb")

        exchange_curvature()
        for other, to in plane():
            put(q.at[other], xyr.at[j], "s_xy", "r_xy", to)
        xyr[j] = q[j]
        alpha = jnp.where(it == 0, -1.0, vals[0] / curvature())
        got(xyr.at[pl.ds(0, XY - 1)], "r_xy")
        total = jnp.sum(xyr[...], axis=0) + weight[...] * weight[...] * rown[...]
        gext[HALO + j] = gext[HALO + j] - alpha * total
        for _, to in plane():
            put(gext.at[HALO + j], gext.at[HALO + j], "s_xg", "r_xg", to)
        step_on(alpha)
        got(gext.at[pl.ds(0, XY - 1)], "r_xg")

        def convert(i, square):
            value = gext[pl.ds(HALO + 4 * i, 4)].reshape(160, 128)
            g2[pl.ds(pl.multiple_of(160 * i, 160), 160), :] = halves(value)
            return square + jnp.sum(value * value, axis=0, keepdims=True)

        square = lax.fori_loop(0, 4, convert, jnp.zeros((1, 128), F32))
        snd[0] = square
        put(snd.at[0], pab.at[0], "s_pa", "r_pa", partner)
        forward(1 - c)
        put(part.at[1 - c], pairb, "s_pair", "r_pair", partner)
        forward(c)
        got(pab.at[0], "r_pa")
        sca[z] = square + pab[0]
        got(pairb, "r_pair")

        def add_pair(i, _):
            part[c, i] = part[c, i] + pairb[i]
            return 0

        lax.fori_loop(0, NZ, add_pair, 0)

        mine = part.at[c]
        for e in (8, 7, 6, 5):
            put(mine.at[ring(e)], relp.at[e - 5], "s_rs", "r_relp", along(e - 4))
            if e < 8:
                put(mine.at[ring(-e)], relm.at[e - 5], "s_rs", "r_relm", along(4 - e))
        for e in (3, 2, 1):
            put(mine.at[ring(e)], dirb.at[e - 1], "s_rs", "r_dir", along(e))
            put(mine.at[ring(-e)], dirb.at[e + 2], "s_rs", "r_dir", along(-e))
        for k in range(1, NZ):
            put(sca.at[z], sca.at[z], "s_sa", "r_sa", along(k))

        @pl.when(j < HALO)
        def _():
            put(gext.at[pl.ds(XY, HALO)], gext.at[pl.ds(0, HALO)], "s_hl", "r_hl", after)

        @pl.when(j >= XY - HALO)
        def _():
            put(gext.at[pl.ds(HALO, HALO)], gext.at[pl.ds(HALO + XY, HALO)], "s_hr", "r_hr", before)

        got(relp, "r_relp")
        part[c, ring(4)] = part[c, ring(4)] + jnp.sum(relp[...], axis=0)
        put(mine.at[ring(4)], fin.at[0], "s_rs", "r_fin", along(4))
        got(relm, "r_relm")
        part[c, ring(-4)] = part[c, ring(-4)] + jnp.sum(relm[...], axis=0)
        put(mine.at[ring(-4)], fin.at[1], "s_rs", "r_fin", along(-4))

        got(sca.at[pl.ds(0, NZ - 1)], "r_sa")
        norm = jnp.sum(sca[...], axis=0)
        beta = norm / vals[1]
        vals[0] = norm
        vals[1] = norm
        got(dirb, "r_dir")
        got(fin, "r_fin")
        image = part[c, z] + jnp.sum(dirb[...], axis=0) + jnp.sum(fin[...], axis=0) + beta * imgown[...]
        imgown[...] = image

        @pl.when(it < ITERS - 1)
        def _():
            img[c, z] = image
            for e in (4, 3, 2, 1):
                for way in (e, -e):
                    r = {4: "r_aga", -4: "r_agb"}.get(way, "r_ag6")
                    put(img.at[c, z], img.at[c, z], "s_ag", r, along(way))

        @pl.when(it == 0)
        def _():
            build_l()

        @pl.when(j < HALO)
        def _():
            got(gext.at[pl.ds(0, HALO)], "r_hl")
            sent(gext.at[pl.ds(0, HALO)], "s_hl")

        @pl.when(j >= XY - HALO)
        def _():
            got(gext.at[pl.ds(0, HALO)], "r_hr")
            sent(gext.at[pl.ds(0, HALO)], "s_hr")

        window = gext[pl.ds(j, XY)].reshape(JWIN, 128)
        lg = folded(dot(lx[...], halves(window)))
        rg = folded(dot(lxt[...], halves(lg)))[24 : 24 + R]
        ld = lg[160 : 160 + R] + beta * ldown[...]
        ldown[...] = ld
        rown[...] = rg + beta * rown[...]
        share = jnp.sum(image * image, axis=0, keepdims=True)
        share = share + weight[...] * weight[...] * jnp.sum(ld * ld, axis=0, keepdims=True)
        snd[1] = share
        put(snd.at[1], pab.at[1], "s_pb", "r_pb", partner)

        def turn(i, _):
            d[i] = gext[HALO + i] + beta * d[i]
            return 0

        lax.fori_loop(0, XY, turn, 0)
        got(pab.at[1], "r_pb")
        scb[z] = share + pab[1]
        for k in range(1, NZ):
            put(scb.at[z], scb.at[z], "s_sb", "r_sb", along(k))

        @pl.when(it < ITERS - 1)
        def _():
            got(img.at[c, 0], "r_aga")
            for e in (4, 3, 2, 1):
                put(img.at[c, ring(-4)], img.at[c, ring(-4)], "s_ag", "r_ag7", along(e))
            got(img.at[c, 0], "r_agb")
            for e in (3, 2, 1):
                put(img.at[c, ring(4)], img.at[c, ring(4)], "s_ag", "r_ag7", along(-e))
            got(img.at[c, pl.ds(0, 6)], "r_ag6")
            got(img.at[c, pl.ds(0, 7)], "r_ag7")
            put(img.at[c], img.at[c], "s_pag", "r_pag", partner)
            sent(img.at[c, pl.ds(0, 15)], "s_ag")

        sent(xyr.at[pl.ds(0, XY - 1)], "s_xy")
        sent(xs.at[pl.ds(0, XY - 1)], "s_xs")
        sent(gext.at[pl.ds(0, XY - 1)], "s_xg")
        sent(snd.at[0], "s_pa")
        sent(snd.at[1], "s_pb")
        sent(pairb, "s_pair")
        sent(pairb.at[pl.ds(0, NZ - 1)], "s_rs")
        sent(sca.at[pl.ds(0, NZ - 1)], "s_sa")
        sent(scb.at[pl.ds(0, NZ - 1)], "s_sb")
        return 0

    lax.fori_loop(0, ITERS, body, 0)

    got(scb.at[pl.ds(0, NZ - 1)], "r_sb")
    exchange_curvature()
    step_on(vals[0] / curvature())
    sent(xs.at[pl.ds(0, XY - 1)], "s_xs")
    sent(offl.at[:, pl.ds(0, 2 * OFFH)], "s_off")


def shards(green, data, neighbours, reg_weight):
    rows, cols = green.shape
    chunks = (XY, R, 128)
    vmem = pl.BlockSpec(memory_space=pltpu.VMEM)
    hbm = pl.BlockSpec(memory_space=pl.ANY)
    scratch = [
        ((rows, cols), F32),
        ((rows, cols), BF16), ((rows, cols), BF16), ((cols, rows), BF16), ((cols, rows), BF16),
        ((640, 256), BF16), ((640, 256), BF16),
        ((2, *chunks), F32), (chunks, F32),
        ((4, R, 128), F32), ((3, R, 128), F32), ((6, R, 128), F32), ((2, R, 128), F32),
        ((2, *chunks), F32), (chunks, F32), (chunks, F32),
        ((2 * HALO + XY + 1, R, 128), F32), (chunks, F32),
        ((R, 128), F32), ((R, 128), F32), ((R, 128), F32),
        ((8, 2 * OFFH + cols), F32), ((KWIN, JWIN), BF16), ((128, KWIN), BF16),
        ((NZ, 1, 128), F32), ((NZ, 1, 128), F32), ((XY, 1, 128), F32),
        ((2, 1, 128), F32), ((2, 1, 128), F32), ((2, 1, 128), F32),
    ]
    result = pl.pallas_call(
        kernel,
        out_shape=jax.ShapeDtypeStruct(chunks, F32),
        in_specs=[hbm, hbm, vmem, vmem],
        out_specs=vmem,
        scratch_shapes=[pltpu.VMEM(shape, kind) for shape, kind in scratch]
        + [pltpu.SemaphoreType.DMA((len(SEMS),))],
        compiler_params=pltpu.CompilerParams(
            collective_id=0, has_side_effects=True, vmem_limit_bytes=48 * 1024 * 1024
        ),
    )(green, data.reshape(2, *chunks), neighbours, reg_weight.reshape(1, 128))
    return result.reshape(cols, 128)


def solution(mesh):
    whole = Mesh(mesh.devices.reshape(NX, NY, NZ, 2), ("x", "y", "z", "c"))
    in_specs = (P(OBS, PATCH), P(OBS, None), P(None, PATCH), P())
    return jax.shard_map(
        shards, mesh=whole, in_specs=in_specs, out_specs=P(PATCH, None), check_vma=False
    )
```

time: 762 us -> 156 us (0.20); the launches traced: 752 us -> 155 us
  blocking collectives: 309 us -> 0 us
  waiting for transfers between devices: 211 us -> 0 us
  Pallas kernels: 0 us -> 150 us
  other arithmetic: 74.5 us -> 0 us
  starting transfers between devices: 58.8 us -> 0 us
  local copies, waits for them, and re-layouts: 61.7 us -> 5.1 us
  matrix products: 22.9 us -> 0 us
  between operations: 13.6 us -> 0.01 us
    psum x12 -> x0, blocking collectives: 157 us -> none  [over_axes_2(): shard = lax.psum(shard, axis)]
    pallas_call x0 -> x1, Pallas kernels: none -> 150 us  [shards(): pl.pallas_call(kernel, out_shape=jax.ShapeDtypeStruct(chunks, F32), in_sp...]
    all_gather x3 -> x0, waiting for transfers between devices: 137 us -> none  [total_of_pieces(): pieces = lax.all_gather(shard, axis)]
    all_gather x6 -> x0, blocking collectives: 102 us -> none  [all_blocks(): pieces = lax.all_gather(pieces, axes[k], axis=0, tiled=True)]
    ppermute x10 -> x0, waiting for transfers between devices: 69.5 us -> none  [the longest x3 55.1 us: extended_2(): before = lax.ppermute(last, axis, up)]
    all_to_all x2 -> x0, blocking collectives: 49.6 us -> none  [sent_to_all(): lax.all_to_all(jnp.broadcast_to(shard[None], (length, *shard.shape)), axi...]
    scatter-add x6 -> x0, other arithmetic: 45 us -> none  [shards(): spread = spread.at[local_ids[slot]].add(reg_resid)]
    all_to_all x4 -> x0, starting transfers between devices: 31.3 us -> none  [the longest x3 18.1 us: summed_on_arrival(): lax.all_to_all(cut_along(shard, dim, length), axis, 0, 0, tiled=True)]
  transfers between devices with their start and end apart: 17 -> 0, of which waited for: 10 -> 0; matrix products, arithmetic and copies ran while one was open for 15% -> 0% of each run, Pallas kernels for 0% -> 0%
where the time goes in v1:
time: 156 us; the launch traced here: 155 us
  Pallas kernels  150 us (96%)
  local copies, waits for them, and re-layouts  5.1 us (3%)
    pallas_call x1, Pallas kernels, shards(): pl.pallas_call(kernel, out_shape=jax.ShapeDtypeStruct(chunks, F32), in_sp...  150 us
    unnamed x9, local copies, waits for them, and re-layouts  5.1 us

profile of v1, /device:TPU:1, one launch (start us, length us, event | category | flops | bytes accessed | tf_op | source)
XLA Modules:
  0.0 155.5 jit_solution(11253370489972110326)
XLA Ops:
  0.0 0.0 copy-start
  0.0 1.9 %copy-done = f32[1280,640]{1,0:T(8,128)S(1)} copy-done((f32[1280,640]{1,0:T(8,128)S(1)}, f32[1280,640]{1,0:T(8,128)}, u32[]{:S(2)}) %copy-start) | copy-done | bytes 3276824
  1.9 0.0 copy-start.1
  1.9 1.1 copy-done.1
  3.0 0.0 copy-start.2
  3.0 0.7 copy-done.2
  3.7 0.0 copy-start.3
  3.7 0.7 copy-done.3
  4.4 150.4 %shard_map.46 = f32[16,40,128]{2,1,0:T(8,128)S(1)} custom-call(f32[1280,640]{1,0:T(8,128)S(1)} %copy-done, f32[2,16,40,128]{3,2,1,0:T(8,128)S(1)} %bitcast.4, s32[3,640]{1,0:T(4,128)S(1)} %copy-done.2, f32[1,128]{1,0:T(1,128)S(1)} %bitcast.5), custom_call_target="tpu_custom_call" | custom-call | tf_op jit(solution)/shard_map/pallas_call | solution.py:382
  154.7 0.7 copy.6
Async XLA Ops:
  0.0 1.9 %copy-start = (f32[1280,640]{1,0:T(8,128)S(1)}, f32[1280,640]{1,0:T(8,128)}, u32[]{:S(2)}) copy-start(f32[1280,640]{1,0:T(8,128)} %green.1) | copy-start | bytes 9830404
  1.9 1.1 copy-start.1
  3.0 0.7 copy-start.2
  3.7 0.7 copy-start.3

commit v2 on v1

--- a/solution.py
+++ b/solution.py
@@ -21,12 +21,22 @@
 OFFH = 256
 
 SEMS = (
-    ["g0", "g1", "g2", "g3", "g4", "data", "s_off", "r_offl", "r_offr", "s_xy", "r_xy", "s_xs", "r_xs", "s_xg", "r_xg"]
+    ["g0", "g1", "g2", "g3", "g4", "data", "nb", "w", "s_off", "r_offl", "r_offr", "s_xy", "r_xy", "s_xs", "r_xs", "s_xg", "r_xg"]
     + ["s_pa", "r_pa", "s_pair", "r_pair", "s_rs", "r_relp", "r_relm", "r_dir", "r_fin", "s_sa", "r_sa"]
-    + ["s_hl", "s_hr", "r_hl", "r_hr", "s_ag", "r_aga", "r_agb", "r_ag6", "r_ag7", "s_pb", "r_pb", "s_sb", "r_sb"]
+    + ["s_hl", "s_hr", "r_hl", "r_hr", "s_ag", "r_aga", "r_agb", "r_ag6", "r_ag7", "s_sb", "r_sb"]
     + ["s_pag", "r_pag"]
 )
 SEM = {name: place for place, name in enumerate(SEMS)}
+
+
+def hops(offset):
+    return sum(min(step, size - step) for step, size in zip(offset, (NX, NY)))
+
+
+FAR_RING = sorted(range(1, NZ), key=lambda k: min(k, NZ - k), reverse=True)
+FARTHEST_FIRST = sorted(
+    ((dx, dy) for dx in range(NX) for dy in range(NY) if dx or dy), key=hops, reverse=True
+)
 
 
 def split(value):
@@ -48,9 +58,9 @@
 
 
 def kernel(
-    green, data, neighbours, weight, out,
+    green, data, neighbours, reg_weight, out,
     gf, ghi, glo, thi, tlo, g2, im2, part, pairb, relp, relm, dirb, fin, img, q, xyr, gext, d,
-    imgown, ldown, rown, offl, lx, lxt, sca, scb, xs, pab, snd, vals, sems,
+    imgown, ldown, rown, offl, lx, lxt, sca, scb, xs, pab, snd, vals, table, weight, sems,
 ):
     x, y, z, c = (lax.axis_index(a) for a in ("x", "y", "z", "c"))
     j = x * NY + y
@@ -70,11 +80,9 @@
     after = (x, y, wrapped(z + c), 1 - c)
 
     def plane():
-        for dx in range(NX):
-            for dy in range(NY):
-                if dx or dy:
-                    px, py = lax.rem(x + dx, NX), lax.rem(y + dy, NY)
-                    yield px * NY + py, (px, py, z, c)
+        for dx, dy in FARTHEST_FIRST:
+            px, py = lax.rem(x + dx, NX), lax.rem(y + dy, NY)
+            yield px * NY + py, (px, py, z, c)
 
     def copy(src, dst, s, r, to):
         return pltpu.make_async_remote_copy(
@@ -96,38 +104,40 @@
         for i in range(5)
     ]
     load_data = pltpu.make_async_copy(data, img, sems.at[SEM["data"]])
+    load_table = pltpu.make_async_copy(neighbours, table, sems.at[SEM["nb"]])
+    load_weight = pltpu.make_async_copy(reg_weight, weight, sems.at[SEM["w"]])
+    load_table.start()
     for load in loads:
         load.start()
     load_data.start()
+    load_weight.start()
 
     cols = neighbours.shape[1]
     base = (2 * z + c) * cols
-    ids = base + lax.broadcasted_iota(jnp.int32, neighbours.shape, 1)
-    offl[...] = jnp.zeros_like(offl)
-    offl[0:3, OFFH : OFFH + cols] = (neighbours[...] - ids).astype(F32)
-    for ref in (gext, d, imgown, ldown, rown, sca, scb, xs, vals):
+    for ref in (gext, d, imgown, ldown, rown, sca, scb, xs, offl):
         ref[...] = jnp.zeros_like(ref)
-    out[...] = jnp.zeros_like(out)
+    vals[0:1] = jnp.full((1, 1, 128), -1.0, F32)
     vals[1:2] = jnp.ones((1, 1, 128), F32)
+    load_table.wait()
+    ids = base + lax.broadcasted_iota(jnp.int32, table.shape, 1)
+    offl[0:3, OFFH : OFFH + cols] = (table[...] - ids).astype(F32)
 
     barrier = pltpu.get_barrier_semaphore()
     greeted = [along(k) for k in range(1, NZ)] + [to for _, to in plane()]
-    greeted += [partner, (x, y, wrapped(z - 1 + 2 * c), 1 - c)]
+    greeted += [partner] + [(x, y, ring(k), 1 - c) for k in range(1, NZ)]
     for to in greeted:
         pl.semaphore_signal(barrier, inc=1, device_id=to, device_id_type=MESH)
 
+    out[...] = jnp.zeros_like(out)
     for i in range(5):
         loads[i].wait()
         for k in range(2):
-            rows = pl.ds(256 * i + 128 * k, 128)
-            block = gf[rows, :]
-            ghi[rows, :], glo[rows, :] = split(block)
-            thi[:, rows], tlo[:, rows] = split(block.T)
+            place = 2 * i + k
+            high, low = split(gf[pl.ds(128 * place, 128), :].T)
+            half, columns = place // 5, pl.ds(128 * (place % 5), 128)
+            thi[half, :, columns], tlo[half, :, columns] = high, low
+    load_weight.wait()
     load_data.wait()
-
-    pl.semaphore_wait(barrier, len(greeted))
-    put(offl.at[:, pl.ds(cols, OFFH)], offl.at[:, pl.ds(0, OFFH)], "s_off", "r_offl", after)
-    put(offl.at[:, pl.ds(OFFH, OFFH)], offl.at[:, pl.ds(OFFH + cols, OFFH)], "s_off", "r_offr", before)
 
     def forward(half):
         def tile(i, _):
@@ -145,11 +155,9 @@
             return 0
 
         lax.fori_loop(0, 4, convert, 0)
-        depth = pl.ds(pl.multiple_of(half * 640, 128), 640)
-
         def tile(i, _):
             rows = pl.ds(pl.multiple_of(i * 160, 160), 160)
-            both = dot(thi[rows, depth], im2[...]) + dot(tlo[rows, depth], im2[...])
+            both = dot(thi[half, rows, :], im2[...]) + dot(tlo[half, rows, :], im2[...])
             value = folded(both).reshape(4, R, 128)
             place = pl.ds(4 * i, 4)
             q[place] = q[place] + value if add else value
@@ -157,7 +165,16 @@
 
         lax.fori_loop(0, 4, tile, 0)
 
+    def split_rows():
+        def tile(i, _):
+            rows = pl.ds(pl.multiple_of(i * 128, 128), 128)
+            ghi[rows, :], glo[rows, :] = split(gf[rows, :])
+            return 0
+
+        lax.fori_loop(0, 10, tile, 0)
+
     def exchange_curvature():
+        got(scb.at[pl.ds(0, 2 * NZ - 1)], "r_sb")
         xs[pl.ds(j, 1)] = jnp.sum(scb[...], axis=0, keepdims=True)
         for _, to in plane():
             put(xs.at[j], xs.at[j], "s_xs", "r_xs", to)
@@ -213,13 +230,27 @@
         @pl.when(it > 0)
         def _():
             sent(img.at[0], "s_pag")
-            got(scb.at[pl.ds(0, NZ - 1)], "r_sb")
-
-        exchange_curvature()
+
+        @pl.when(it == 0)
+        def _():
+            pl.semaphore_wait(barrier, len(greeted))
+            put(offl.at[:, pl.ds(cols, OFFH)], offl.at[:, pl.ds(0, OFFH)], "s_off", "r_offl", after)
+            put(offl.at[:, pl.ds(OFFH, OFFH)], offl.at[:, pl.ds(OFFH + cols, OFFH)], "s_off", "r_offr", before)
+
         for other, to in plane():
             put(q.at[other], xyr.at[j], "s_xy", "r_xy", to)
         xyr[j] = q[j]
-        alpha = jnp.where(it == 0, -1.0, vals[0] / curvature())
+
+        @pl.when(it > 0)
+        def _():
+            exchange_curvature()
+            vals[0] = vals[1] / curvature()
+
+        @pl.when(it == 0)
+        def _():
+            split_rows()
+
+        alpha = vals[0]
         got(xyr.at[pl.ds(0, XY - 1)], "r_xy")
         total = jnp.sum(xyr[...], axis=0) + weight[...] * weight[...] * rown[...]
         gext[HALO + j] = gext[HALO + j] - alpha * total
@@ -227,6 +258,14 @@
             put(gext.at[HALO + j], gext.at[HALO + j], "s_xg", "r_xg", to)
         step_on(alpha)
         got(gext.at[pl.ds(0, XY - 1)], "r_xg")
+
+        @pl.when(j < HALO)
+        def _():
+            put(gext.at[pl.ds(XY, HALO)], gext.at[pl.ds(0, HALO)], "s_hl", "r_hl", after)
+
+        @pl.when(j >= XY - HALO)
+        def _():
+            put(gext.at[pl.ds(HALO, HALO)], gext.at[pl.ds(HALO + XY, HALO)], "s_hr", "r_hr", before)
 
         def convert(i, square):
             value = gext[pl.ds(HALO + 4 * i, 4)].reshape(160, 128)
@@ -257,16 +296,8 @@
         for e in (3, 2, 1):
             put(mine.at[ring(e)], dirb.at[e - 1], "s_rs", "r_dir", along(e))
             put(mine.at[ring(-e)], dirb.at[e + 2], "s_rs", "r_dir", along(-e))
-        for k in range(1, NZ):
+        for k in FAR_RING:
             put(sca.at[z], sca.at[z], "s_sa", "r_sa", along(k))
-
-        @pl.when(j < HALO)
-        def _():
-            put(gext.at[pl.ds(XY, HALO)], gext.at[pl.ds(0, HALO)], "s_hl", "r_hl", after)
-
-        @pl.when(j >= XY - HALO)
-        def _():
-            put(gext.at[pl.ds(HALO, HALO)], gext.at[pl.ds(HALO + XY, HALO)], "s_hr", "r_hr", before)
 
         got(relp, "r_relp")
         part[c, ring(4)] = part[c, ring(4)] + jnp.sum(relp[...], axis=0)
@@ -275,10 +306,27 @@
         part[c, ring(-4)] = part[c, ring(-4)] + jnp.sum(relm[...], axis=0)
         put(mine.at[ring(-4)], fin.at[1], "s_rs", "r_fin", along(-4))
 
+        @pl.when(it == 0)
+        def _():
+            build_l()
+
+        @pl.when(j < HALO)
+        def _():
+            got(gext.at[pl.ds(0, HALO)], "r_hl")
+            sent(gext.at[pl.ds(0, HALO)], "s_hl")
+
+        @pl.when(j >= XY - HALO)
+        def _():
+            got(gext.at[pl.ds(0, HALO)], "r_hr")
+            sent(gext.at[pl.ds(0, HALO)], "s_hr")
+
+        window = gext[pl.ds(j, XY)].reshape(JWIN, 128)
+        lg = folded(dot(lx[...], halves(window)))
+        rg = folded(dot(lxt[...], halves(lg)))[24 : 24 + R]
+
         got(sca.at[pl.ds(0, NZ - 1)], "r_sa")
         norm = jnp.sum(sca[...], axis=0)
         beta = norm / vals[1]
-        vals[0] = norm
         vals[1] = norm
         got(dirb, "r_dir")
         got(fin, "r_fin")
@@ -293,41 +341,13 @@
                     r = {4: "r_aga", -4: "r_agb"}.get(way, "r_ag6")
                     put(img.at[c, z], img.at[c, z], "s_ag", r, along(way))
 
-        @pl.when(it == 0)
-        def _():
-            build_l()
-
-        @pl.when(j < HALO)
-        def _():
-            got(gext.at[pl.ds(0, HALO)], "r_hl")
-            sent(gext.at[pl.ds(0, HALO)], "s_hl")
-
-        @pl.when(j >= XY - HALO)
-        def _():
-            got(gext.at[pl.ds(0, HALO)], "r_hr")
-            sent(gext.at[pl.ds(0, HALO)], "s_hr")
-
-        window = gext[pl.ds(j, XY)].reshape(JWIN, 128)
-        lg = folded(dot(lx[...], halves(window)))
-        rg = folded(dot(lxt[...], halves(lg)))[24 : 24 + R]
         ld = lg[160 : 160 + R] + beta * ldown[...]
         ldown[...] = ld
         rown[...] = rg + beta * rown[...]
         share = jnp.sum(image * image, axis=0, keepdims=True)
         share = share + weight[...] * weight[...] * jnp.sum(ld * ld, axis=0, keepdims=True)
-        snd[1] = share
-        put(snd.at[1], pab.at[1], "s_pb", "r_pb", partner)
-
-        def turn(i, _):
-            d[i] = gext[HALO + i] + beta * d[i]
-            return 0
-
-        lax.fori_loop(0, XY, turn, 0)
-        got(pab.at[1], "r_pb")
-        scb[z] = share + pab[1]
-        for k in range(1, NZ):
-            put(scb.at[z], scb.at[z], "s_sb", "r_sb", along(k))
-
+        place = 2 * z + c
+        scb[place] = share
         @pl.when(it < ITERS - 1)
         def _():
             got(img.at[c, 0], "r_aga")
@@ -336,27 +356,40 @@
             got(img.at[c, 0], "r_agb")
             for e in (3, 2, 1):
                 put(img.at[c, ring(4)], img.at[c, ring(4)], "s_ag", "r_ag7", along(-e))
+
+        for to in [along(k) for k in FAR_RING] + [(x, y, ring(k), 1 - c) for k in FAR_RING] + [partner]:
+            put(scb.at[place], scb.at[place], "s_sb", "r_sb", to)
+
+        def turn(i, _):
+            d[i] = gext[HALO + i] + beta * d[i]
+            return 0
+
+        lax.fori_loop(0, XY, turn, 0)
+
+        @pl.when(it < ITERS - 1)
+        def _():
             got(img.at[c, pl.ds(0, 6)], "r_ag6")
             got(img.at[c, pl.ds(0, 7)], "r_ag7")
             put(img.at[c], img.at[c], "s_pag", "r_pag", partner)
             sent(img.at[c, pl.ds(0, 15)], "s_ag")
 
         sent(xyr.at[pl.ds(0, XY - 1)], "s_xy")
-        sent(xs.at[pl.ds(0, XY - 1)], "s_xs")
+        @pl.when(it > 0)
+        def _():
+            sent(xs.at[pl.ds(0, XY - 1)], "s_xs")
+
         sent(gext.at[pl.ds(0, XY - 1)], "s_xg")
         sent(snd.at[0], "s_pa")
-        sent(snd.at[1], "s_pb")
         sent(pairb, "s_pair")
         sent(pairb.at[pl.ds(0, NZ - 1)], "s_rs")
         sent(sca.at[pl.ds(0, NZ - 1)], "s_sa")
-        sent(scb.at[pl.ds(0, NZ - 1)], "s_sb")
+        sent(scb.at[pl.ds(0, 2 * NZ - 1)], "s_sb")
         return 0
 
     lax.fori_loop(0, ITERS, body, 0)
 
-    got(scb.at[pl.ds(0, NZ - 1)], "r_sb")
     exchange_curvature()
-    step_on(vals[0] / curvature())
+    step_on(vals[1] / curvature())
     sent(xs.at[pl.ds(0, XY - 1)], "s_xs")
     sent(offl.at[:, pl.ds(0, 2 * OFFH)], "s_off")
 
@@ -365,10 +398,10 @@
     rows, cols = green.shape
     chunks = (XY, R, 128)
     vmem = pl.BlockSpec(memory_space=pltpu.VMEM)
-    hbm = pl.BlockSpec(memory_space=pl.ANY)
+    hbm = pl.BlockSpec(memory_space=pltpu.HBM)
     scratch = [
         ((rows, cols), F32),
-        ((rows, cols), BF16), ((rows, cols), BF16), ((cols, rows), BF16), ((cols, rows), BF16),
+        ((rows, cols), BF16), ((rows, cols), BF16), ((2, cols, cols), BF16), ((2, cols, cols), BF16),
         ((640, 256), BF16), ((640, 256), BF16),
         ((2, *chunks), F32), (chunks, F32),
         ((4, R, 128), F32), ((3, R, 128), F32), ((6, R, 128), F32), ((2, R, 128), F32),
@@ -376,18 +409,18 @@
         ((2 * HALO + XY + 1, R, 128), F32), (chunks, F32),
         ((R, 128), F32), ((R, 128), F32), ((R, 128), F32),
         ((8, 2 * OFFH + cols), F32), ((KWIN, JWIN), BF16), ((128, KWIN), BF16),
-        ((NZ, 1, 128), F32), ((NZ, 1, 128), F32), ((XY, 1, 128), F32),
-        ((2, 1, 128), F32), ((2, 1, 128), F32), ((2, 1, 128), F32),
+        ((NZ, 1, 128), F32), ((2 * NZ, 1, 128), F32), ((XY, 1, 128), F32),
+        ((1, 1, 128), F32), ((1, 1, 128), F32), ((2, 1, 128), F32),
     ]
     result = pl.pallas_call(
         kernel,
         out_shape=jax.ShapeDtypeStruct(chunks, F32),
-        in_specs=[hbm, hbm, vmem, vmem],
+        in_specs=[hbm] * 4,
         out_specs=vmem,
         scratch_shapes=[pltpu.VMEM(shape, kind) for shape, kind in scratch]
-        + [pltpu.SemaphoreType.DMA((len(SEMS),))],
+        + [pltpu.VMEM(neighbours.shape, jnp.int32), pltpu.VMEM((1, 128), F32), pltpu.SemaphoreType.DMA((len(SEMS),))],
         compiler_params=pltpu.CompilerParams(
-            collective_id=0, has_side_effects=True, vmem_limit_bytes=48 * 1024 * 1024
+            collective_id=0, has_side_effects=True, vmem_limit_bytes=67_000_000
         ),
     )(green, data.reshape(2, *chunks), neighbours, reg_weight.reshape(1, 128))
     return result.reshape(cols, 128)

time: 156 us -> 146 us (0.936)
  Pallas kernels: 150 us -> 144 us
  local copies, waits for them, and re-layouts: 5.1 us -> 1.72 us
    pallas_call x1, Pallas kernels: 150 us -> 144 us  [shards(): pl.pallas_call(kernel, out_shape=jax.ShapeDtypeStruct(chunks, F32), in_sp...]
    unnamed x9 -> x1, local copies, waits for them, and re-layouts: 5.1 us -> 1.72 us
where the time goes in v2:
time: 146 us
  Pallas kernels  144 us (99%)
  local copies, waits for them, and re-layouts  1.72 us (1%)
    pallas_call x1, Pallas kernels, shards(): pl.pallas_call(kernel, out_shape=jax.ShapeDtypeStruct(chunks, F32), in_sp...  144 us

profile of v2, /device:TPU:1, one launch (start us, length us, event | category | flops | bytes accessed | tf_op | source)
XLA Modules:
  0.0 146.2 jit_solution(9972037466109046204)
XLA Ops:
  0.0 144.4 %shard_map.46 = f32[16,40,128]{2,1,0:T(8,128)} custom-call(f32[1280,640]{1,0:T(8,128)} %green.1, f32[2,16,40,128]{3,2,1,0:T(8,128)} %bitcast.4, s32[3,640]{1,0:T(4,128)} %neighbours.1, f32[1,128]{1,0:T(1,128)} %bitcast.5), custom_call_target="tpu_custom_call" | custom-call | tf_op jit(solution)/shard_map/pallas_call | solution.py:415
  144.4 1.7 %copy.6 = f32[640,128]{1,0:T(8,128)} copy(f32[640,128]{1,0:T(8,128)} %bitcast.3) | data formatting | bytes 655360

commit v3 on v2

--- a/solution.py
+++ b/solution.py
@@ -22,8 +22,8 @@
 
 SEMS = (
     ["g0", "g1", "g2", "g3", "g4", "data", "nb", "w", "s_off", "r_offl", "r_offr", "s_xy", "r_xy", "s_xs", "r_xs", "s_xg", "r_xg"]
-    + ["s_pa", "r_pa", "s_pair", "r_pair", "s_rs", "r_relp", "r_relm", "r_dir", "r_fin", "s_sa", "r_sa"]
-    + ["s_hl", "s_hr", "r_hl", "r_hr", "s_ag", "r_aga", "r_agb", "r_ag6", "r_ag7", "s_sb", "r_sb"]
+    + ["s_pa", "r_pa", "s_pair", "r_pair", "s_rs", "r_6p", "r_6m", "r_3p", "r_3m", "r_dir", "r_fin", "s_sa", "r_sa"]
+    + ["s_hl", "s_hr", "r_hl", "r_hr", "s_ag", "r_a3p", "r_a3m", "r_a6p", "r_a6m", "r_ad", "r_ax", "s_sb", "r_sb"]
     + ["s_pag", "r_pag"]
 )
 SEM = {name: place for place, name in enumerate(SEMS)}
@@ -59,8 +59,8 @@
 
 def kernel(
     green, data, neighbours, reg_weight, out,
-    gf, ghi, glo, thi, tlo, g2, im2, part, pairb, relp, relm, dirb, fin, img, q, xyr, gext, d,
-    imgown, ldown, rown, offl, lx, lxt, sca, scb, xs, pab, snd, vals, table, weight, sems,
+    gf, ghi, glo, thi, tlo, g2, im2, part, pairb, at6p, at6m, at3p, at3m, dirb, fin, img, q, xyr, gext, d,
+    imgown, ldown, rown, offl, lx, lxt, sca, scb, xs, pab, snd, vals, table, weight, sems, known,
 ):
     x, y, z, c = (lax.axis_index(a) for a in ("x", "y", "z", "c"))
     j = x * NY + y
@@ -123,8 +123,8 @@
     offl[0:3, OFFH : OFFH + cols] = (table[...] - ids).astype(F32)
 
     barrier = pltpu.get_barrier_semaphore()
-    greeted = [along(k) for k in range(1, NZ)] + [to for _, to in plane()]
-    greeted += [partner] + [(x, y, ring(k), 1 - c) for k in range(1, NZ)]
+    greeted = [to for _, to in plane()] + [partner, along(1), along(-1)]
+    greeted += [(x, y, wrapped(z - 1 + 2 * c), 1 - c)]
     for to in greeted:
         pl.semaphore_signal(barrier, inc=1, device_id=to, device_id_type=MESH)
 
@@ -139,6 +139,13 @@
     load_weight.wait()
     load_data.wait()
 
+    def tell(doubling):
+        for way in (1, -1):
+            pl.semaphore_signal(known.at[doubling], inc=1, device_id=along(way * 2**doubling), device_id_type=MESH)
+
+    def hear(doubling):
+        pl.semaphore_wait(known.at[doubling], 2)
+
     def forward(half):
         def tile(i, _):
             rows = pl.ds(pl.multiple_of(half * 640 + i * 160, 160), 160)
@@ -148,7 +155,7 @@
 
         lax.fori_loop(0, 4, tile, 0)
 
-    def back(half, add):
+    def back(half, last):
         def convert(i, _):
             rows = pl.ds(pl.multiple_of(i * 160, 160), 160)
             im2[rows, :] = halves(img[half, pl.ds(4 * i, 4)].reshape(160, 128))
@@ -156,14 +163,24 @@
 
         lax.fori_loop(0, 4, convert, 0)
         def tile(i, _):
-            rows = pl.ds(pl.multiple_of(i * 160, 160), 160)
+            side = lax.rem(x + 2 + i, NX)
+            rows = pl.ds(pl.multiple_of(side * 160, 160), 160)
             both = dot(thi[half, rows, :], im2[...]) + dot(tlo[half, rows, :], im2[...])
-            value = folded(both).reshape(4, R, 128)
-            place = pl.ds(4 * i, 4)
-            q[place] = q[place] + value if add else value
-            return 0
-
-        lax.fori_loop(0, 4, tile, 0)
+            value = folded(both).reshape(NY, R, 128)
+            place = pl.ds(NY * side, NY)
+            q[place] = q[place] + value if last else value
+            if last:
+                for step in (2, 1, 3, 0):
+                    py = lax.rem(y + step, NY)
+                    other = NY * side + py
+
+                    @pl.when(other != j)
+                    def _():
+                        put(q.at[other], xyr.at[j], "s_xy", "r_xy", (side, py, z, c))
+
+            return 0
+
+        lax.fori_loop(0, NX, tile, 0)
 
     def split_rows():
         def tile(i, _):
@@ -225,20 +242,19 @@
         def _():
             got(img.at[0], "r_pag")
 
-        back(1 - c, True)
-
-        @pl.when(it > 0)
-        def _():
-            sent(img.at[0], "s_pag")
-
         @pl.when(it == 0)
         def _():
             pl.semaphore_wait(barrier, len(greeted))
+            tell(0)
             put(offl.at[:, pl.ds(cols, OFFH)], offl.at[:, pl.ds(0, OFFH)], "s_off", "r_offl", after)
             put(offl.at[:, pl.ds(OFFH, OFFH)], offl.at[:, pl.ds(OFFH + cols, OFFH)], "s_off", "r_offr", before)
 
-        for other, to in plane():
-            put(q.at[other], xyr.at[j], "s_xy", "r_xy", to)
+        back(1 - c, True)
+
+        @pl.when(it > 0)
+        def _():
+            sent(img.at[0], "s_pag")
+
         xyr[j] = q[j]
 
         @pl.when(it > 0)
@@ -248,6 +264,8 @@
 
         @pl.when(it == 0)
         def _():
+            hear(0)
+            tell(1)
             split_rows()
 
         alpha = vals[0]
@@ -256,8 +274,17 @@
         gext[HALO + j] = gext[HALO + j] - alpha * total
         for _, to in plane():
             put(gext.at[HALO + j], gext.at[HALO + j], "s_xg", "r_xg", to)
+        @pl.when(it == 0)
+        def _():
+            hear(1)
+            tell(2)
+
         step_on(alpha)
         got(gext.at[pl.ds(0, XY - 1)], "r_xg")
+
+        @pl.when(it == 0)
+        def _():
+            hear(2)
 
         @pl.when(j < HALO)
         def _():
@@ -277,9 +304,11 @@
         put(snd.at[0], pab.at[0], "s_pa", "r_pa", partner)
         forward(1 - c)
         put(part.at[1 - c], pairb, "s_pair", "r_pair", partner)
-        forward(c)
         got(pab.at[0], "r_pa")
         sca[z] = square + pab[0]
+        for k in FAR_RING:
+            put(sca.at[z], sca.at[z], "s_sa", "r_sa", along(k))
+        forward(c)
         got(pairb, "r_pair")
 
         def add_pair(i, _):
@@ -289,22 +318,18 @@
         lax.fori_loop(0, NZ, add_pair, 0)
 
         mine = part.at[c]
-        for e in (8, 7, 6, 5):
-            put(mine.at[ring(e)], relp.at[e - 5], "s_rs", "r_relp", along(e - 4))
-            if e < 8:
-                put(mine.at[ring(-e)], relm.at[e - 5], "s_rs", "r_relm", along(4 - e))
-        for e in (3, 2, 1):
-            put(mine.at[ring(e)], dirb.at[e - 1], "s_rs", "r_dir", along(e))
-            put(mine.at[ring(-e)], dirb.at[e + 2], "s_rs", "r_dir", along(-e))
-        for k in FAR_RING:
-            put(sca.at[z], sca.at[z], "s_sa", "r_sa", along(k))
-
-        got(relp, "r_relp")
-        part[c, ring(4)] = part[c, ring(4)] + jnp.sum(relp[...], axis=0)
-        put(mine.at[ring(4)], fin.at[0], "s_rs", "r_fin", along(4))
-        got(relm, "r_relm")
-        part[c, ring(-4)] = part[c, ring(-4)] + jnp.sum(relm[...], axis=0)
-        put(mine.at[ring(-4)], fin.at[1], "s_rs", "r_fin", along(-4))
+        relays = ((1, 6, at6p, "r_6p"), (-1, 6, at6m, "r_6m"), (1, 3, at3p, "r_3p"), (-1, 3, at3m, "r_3m"))
+        for way, near, held, name in relays:
+            for e in range(near + held.shape[0], near, -1):
+                put(mine.at[ring(way * e)], held.at[e - near - 1], "s_rs", name, along(way * (e - near)))
+        for e in (2, 1):
+            for way in (1, -1):
+                put(mine.at[ring(way * e)], dirb.at[e - way], "s_rs", "r_dir", along(way * e))
+        for place, (way, near, held, name) in enumerate(relays):
+            got(held, name)
+            target = ring(way * near)
+            part[c, target] = part[c, target] + jnp.sum(held[...], axis=0)
+            put(mine.at[target], fin.at[place], "s_rs", "r_fin", along(way * near))
 
         @pl.when(it == 0)
         def _():
@@ -336,10 +361,9 @@
         @pl.when(it < ITERS - 1)
         def _():
             img[c, z] = image
-            for e in (4, 3, 2, 1):
-                for way in (e, -e):
-                    r = {4: "r_aga", -4: "r_agb"}.get(way, "r_ag6")
-                    put(img.at[c, z], img.at[c, z], "s_ag", r, along(way))
+            for e, name in ((6, "r_a6"), (3, "r_a3"), (2, "r_ad"), (1, "r_ad")):
+                for way, side in ((1, "p"), (-1, "m")):
+                    put(img.at[c, z], img.at[c, z], "s_ag", name + side if e > 2 else name, along(way * e))
 
         ld = lg[160 : 160 + R] + beta * ldown[...]
         ldown[...] = ld
@@ -350,12 +374,11 @@
         scb[place] = share
         @pl.when(it < ITERS - 1)
         def _():
-            got(img.at[c, 0], "r_aga")
-            for e in (4, 3, 2, 1):
-                put(img.at[c, ring(-4)], img.at[c, ring(-4)], "s_ag", "r_ag7", along(e))
-            got(img.at[c, 0], "r_agb")
-            for e in (3, 2, 1):
-                put(img.at[c, ring(4)], img.at[c, ring(4)], "s_ag", "r_ag7", along(-e))
+            for way, far, last, name in ((1, 3, 2, "r_a3p"), (-1, 3, 2, "r_a3m"), (1, 6, 2, "r_a6p"), (-1, 6, 1, "r_a6m")):
+                got(img.at[c, 0], name)
+                held = img.at[c, ring(-far * way)]
+                for e in range(last, 0, -1):
+                    put(held, held, "s_ag", "r_ax", along(way * e))
 
         for to in [along(k) for k in FAR_RING] + [(x, y, ring(k), 1 - c) for k in FAR_RING] + [partner]:
             put(scb.at[place], scb.at[place], "s_sb", "r_sb", to)
@@ -368,8 +391,8 @@
 
         @pl.when(it < ITERS - 1)
         def _():
-            got(img.at[c, pl.ds(0, 6)], "r_ag6")
-            got(img.at[c, pl.ds(0, 7)], "r_ag7")
+            got(img.at[c, pl.ds(0, 4)], "r_ad")
+            got(img.at[c, pl.ds(0, 7)], "r_ax")
             put(img.at[c], img.at[c], "s_pag", "r_pag", partner)
             sent(img.at[c, pl.ds(0, 15)], "s_ag")
 
@@ -404,7 +427,8 @@
         ((rows, cols), BF16), ((rows, cols), BF16), ((2, cols, cols), BF16), ((2, cols, cols), BF16),
         ((640, 256), BF16), ((640, 256), BF16),
         ((2, *chunks), F32), (chunks, F32),
-        ((4, R, 128), F32), ((3, R, 128), F32), ((6, R, 128), F32), ((2, R, 128), F32),
+        ((2, R, 128), F32), ((1, R, 128), F32), ((2, R, 128), F32), ((2, R, 128), F32),
+        ((4, R, 128), F32), ((4, R, 128), F32),
         ((2, *chunks), F32), (chunks, F32), (chunks, F32),
         ((2 * HALO + XY + 1, R, 128), F32), (chunks, F32),
         ((R, 128), F32), ((R, 128), F32), ((R, 128), F32),
@@ -418,7 +442,7 @@
         in_specs=[hbm] * 4,
         out_specs=vmem,
         scratch_shapes=[pltpu.VMEM(shape, kind) for shape, kind in scratch]
-        + [pltpu.VMEM(neighbours.shape, jnp.int32), pltpu.VMEM((1, 128), F32), pltpu.SemaphoreType.DMA((len(SEMS),))],
+        + [pltpu.VMEM(neighbours.shape, jnp.int32), pltpu.VMEM((1, 128), F32), pltpu.SemaphoreType.DMA((len(SEMS),)), pltpu.SemaphoreType.REGULAR((3,))],
         compiler_params=pltpu.CompilerParams(
             collective_id=0, has_side_effects=True, vmem_limit_bytes=67_000_000
         ),

time: 146 us -> 139 us (0.952)
  Pallas kernels: 144 us -> 137 us
    pallas_call x1, Pallas kernels: 144 us -> 137 us  [shards(): pl.pallas_call(kernel, out_shape=jax.ShapeDtypeStruct(chunks, F32), in_sp...]
where the time goes in v3:
time: 139 us
  Pallas kernels  137 us (99%)
  local copies, waits for them, and re-layouts  1.72 us (1%)
    pallas_call x1, Pallas kernels, shards(): pl.pallas_call(kernel, out_shape=jax.ShapeDtypeStruct(chunks, F32), in_sp...  137 us

profile of v3, /device:TPU:1, one launch (start us, length us, event | category | flops | bytes accessed | tf_op | source)
XLA Modules:
  0.0 138.8 jit_solution(18322161761563535355)
XLA Ops:
  0.0 137.1 %shard_map.46 = f32[16,40,128]{2,1,0:T(8,128)} custom-call(f32[1280,640]{1,0:T(8,128)} %green.1, f32[2,16,40,128]{3,2,1,0:T(8,128)} %bitcast.4, s32[3,640]{1,0:T(4,128)} %neighbours.1, f32[1,128]{1,0:T(1,128)} %bitcast.5), custom_call_target="tpu_custom_call" | custom-call | tf_op jit(solution)/shard_map/pallas_call | solution.py:439
  137.1 1.7 %copy.6 = f32[640,128]{1,0:T(8,128)} copy(f32[640,128]{1,0:T(8,128)} %bitcast.3) | data formatting | bytes 655360

commit v4 on v3

--- a/solution.py
+++ b/solution.py
@@ -22,8 +22,8 @@
 
 SEMS = (
     ["g0", "g1", "g2", "g3", "g4", "data", "nb", "w", "s_off", "r_offl", "r_offr", "s_xy", "r_xy", "s_xs", "r_xs", "s_xg", "r_xg"]
-    + ["s_pa", "r_pa", "s_pair", "r_pair", "s_rs", "r_6p", "r_6m", "r_3p", "r_3m", "r_dir", "r_fin", "s_sa", "r_sa"]
-    + ["s_hl", "s_hr", "r_hl", "r_hr", "s_ag", "r_a3p", "r_a3m", "r_a6p", "r_a6m", "r_ad", "r_ax", "s_sb", "r_sb"]
+    + ["s_pa", "r_pa", "s_pair", "r_pair", "s_rs", "r_5p", "r_5m", "r_2p", "r_2m", "r_dir", "r_fin", "s_sa", "r_sa"]
+    + ["s_hl", "s_hr", "r_hl", "r_hr", "s_ag", "r_a2p", "r_a2m", "r_a5p", "r_a5m", "r_ad", "r_ax", "s_sb", "r_sb"]
     + ["s_pag", "r_pag"]
 )
 SEM = {name: place for place, name in enumerate(SEMS)}
@@ -59,7 +59,7 @@
 
 def kernel(
     green, data, neighbours, reg_weight, out,
-    gf, ghi, glo, thi, tlo, g2, im2, part, pairb, at6p, at6m, at3p, at3m, dirb, fin, img, q, xyr, gext, d,
+    gf, ghl, thl, g2, im2, part, pairb, at5p, at5m, at2p, at2m, dirb, fin, img, q, xyr, gext, d,
     imgown, ldown, rown, offl, lx, lxt, sca, scb, xs, pab, snd, vals, table, weight, sems, known,
 ):
     x, y, z, c = (lax.axis_index(a) for a in ("x", "y", "z", "c"))
@@ -67,8 +67,10 @@
     sign = 1 - 2 * c
     partner = (x, y, z, 1 - c)
 
+    places = [lax.rem(z + sign * step + NZ, NZ) for step in range(NZ)]
+
     def ring(step):
-        return lax.rem(z + sign * step + 2 * NZ, NZ)
+        return places[step % NZ]
 
     def along(step):
         return (x, y, ring(step), c)
@@ -79,9 +81,12 @@
     before = (x, y, wrapped(z - 1 + c), 1 - c)
     after = (x, y, wrapped(z + c), 1 - c)
 
+    xs_of = [lax.rem(x + step, NX) for step in range(NX)]
+    ys_of = [lax.rem(y + step, NY) for step in range(NY)]
+
     def plane():
         for dx, dy in FARTHEST_FIRST:
-            px, py = lax.rem(x + dx, NX), lax.rem(y + dy, NY)
+            px, py = xs_of[dx], ys_of[dy]
             yield px * NY + py, (px, py, z, c)
 
     def copy(src, dst, s, r, to):
@@ -134,8 +139,8 @@
         for k in range(2):
             place = 2 * i + k
             high, low = split(gf[pl.ds(128 * place, 128), :].T)
-            half, columns = place // 5, pl.ds(128 * (place % 5), 128)
-            thi[half, :, columns], tlo[half, :, columns] = high, low
+            half, first = place // 5, 128 * (place % 5)
+            thl[half, :, pl.ds(first, 128)], thl[half, :, pl.ds(cols + first, 128)] = high, low
     load_weight.wait()
     load_data.wait()
 
@@ -148,30 +153,32 @@
 
     def forward(half):
         def tile(i, _):
-            rows = pl.ds(pl.multiple_of(half * 640 + i * 160, 160), 160)
-            both = dot(ghi[rows, :], g2[...]) + dot(glo[rows, :], g2[...])
-            part[half, pl.ds(4 * i, 4)] = folded(both).reshape(4, R, 128)
-            return 0
-
-        lax.fori_loop(0, 4, tile, 0)
+            rows = pl.ds(pl.multiple_of(half * 640 + i * 320, 320), 320)
+            both = dot(ghl[rows, :], g2[...])
+            part[half, pl.ds(8 * i, 8)] = folded(both).reshape(8, R, 128)
+            return 0
+
+        lax.fori_loop(0, 2, tile, 0)
 
     def back(half, last):
         def convert(i, _):
             rows = pl.ds(pl.multiple_of(i * 160, 160), 160)
-            im2[rows, :] = halves(img[half, pl.ds(4 * i, 4)].reshape(160, 128))
+            pieces = halves(img[half, pl.ds(4 * i, 4)].reshape(160, 128))
+            im2[rows, :] = pieces
+            im2[pl.ds(pl.multiple_of(cols + i * 160, 160), 160), :] = pieces
             return 0
 
         lax.fori_loop(0, 4, convert, 0)
         def tile(i, _):
             side = lax.rem(x + 2 + i, NX)
             rows = pl.ds(pl.multiple_of(side * 160, 160), 160)
-            both = dot(thi[half, rows, :], im2[...]) + dot(tlo[half, rows, :], im2[...])
+            both = dot(thl[half, rows, :], im2[...])
             value = folded(both).reshape(NY, R, 128)
             place = pl.ds(NY * side, NY)
             q[place] = q[place] + value if last else value
             if last:
                 for step in (2, 1, 3, 0):
-                    py = lax.rem(y + step, NY)
+                    py = ys_of[step]
                     other = NY * side + py
 
                     @pl.when(other != j)
@@ -185,7 +192,7 @@
     def split_rows():
         def tile(i, _):
             rows = pl.ds(pl.multiple_of(i * 128, 128), 128)
-            ghi[rows, :], glo[rows, :] = split(gf[rows, :])
+            ghl[rows, :] = halves(gf[rows, :])
             return 0
 
         lax.fori_loop(0, 10, tile, 0)
@@ -296,7 +303,9 @@
 
         def convert(i, square):
             value = gext[pl.ds(HALO + 4 * i, 4)].reshape(160, 128)
-            g2[pl.ds(pl.multiple_of(160 * i, 160), 160), :] = halves(value)
+            pieces = halves(value)
+            g2[pl.ds(pl.multiple_of(160 * i, 160), 160), :] = pieces
+            g2[pl.ds(pl.multiple_of(cols + 160 * i, 160), 160), :] = pieces
             return square + jnp.sum(value * value, axis=0, keepdims=True)
 
         square = lax.fori_loop(0, 4, convert, jnp.zeros((1, 128), F32))
@@ -311,24 +320,19 @@
         forward(c)
         got(pairb, "r_pair")
 
-        def add_pair(i, _):
-            part[c, i] = part[c, i] + pairb[i]
-            return 0
-
-        lax.fori_loop(0, NZ, add_pair, 0)
-
         mine = part.at[c]
-        relays = ((1, 6, at6p, "r_6p"), (-1, 6, at6m, "r_6m"), (1, 3, at3p, "r_3p"), (-1, 3, at3m, "r_3m"))
+        relays = ((1, 5, at5p, "r_5p"), (-1, 5, at5m, "r_5m"), (1, 2, at2p, "r_2p"), (-1, 2, at2m, "r_2m"))
         for way, near, held, name in relays:
             for e in range(near + held.shape[0], near, -1):
+                part[c, ring(way * e)] = part[c, ring(way * e)] + pairb[ring(way * e)]
                 put(mine.at[ring(way * e)], held.at[e - near - 1], "s_rs", name, along(way * (e - near)))
-        for e in (2, 1):
-            for way in (1, -1):
-                put(mine.at[ring(way * e)], dirb.at[e - way], "s_rs", "r_dir", along(way * e))
+        for place, way in enumerate((1, -1)):
+            part[c, ring(way)] = part[c, ring(way)] + pairb[ring(way)]
+            put(mine.at[ring(way)], dirb.at[place], "s_rs", "r_dir", along(way))
         for place, (way, near, held, name) in enumerate(relays):
             got(held, name)
             target = ring(way * near)
-            part[c, target] = part[c, target] + jnp.sum(held[...], axis=0)
+            part[c, target] = part[c, target] + (pairb[target] + jnp.sum(held[...], axis=0))
             put(mine.at[target], fin.at[place], "s_rs", "r_fin", along(way * near))
 
         @pl.when(it == 0)
@@ -355,15 +359,15 @@
         vals[1] = norm
         got(dirb, "r_dir")
         got(fin, "r_fin")
-        image = part[c, z] + jnp.sum(dirb[...], axis=0) + jnp.sum(fin[...], axis=0) + beta * imgown[...]
+        image = part[c, z] + pairb[z] + jnp.sum(dirb[...], axis=0) + jnp.sum(fin[...], axis=0) + beta * imgown[...]
         imgown[...] = image
 
         @pl.when(it < ITERS - 1)
         def _():
             img[c, z] = image
-            for e, name in ((6, "r_a6"), (3, "r_a3"), (2, "r_ad"), (1, "r_ad")):
+            for e, name in ((5, "r_a5"), (2, "r_a2"), (1, "r_ad")):
                 for way, side in ((1, "p"), (-1, "m")):
-                    put(img.at[c, z], img.at[c, z], "s_ag", name + side if e > 2 else name, along(way * e))
+                    put(img.at[c, z], img.at[c, z], "s_ag", name + side if e > 1 else name, along(way * e))
 
         ld = lg[160 : 160 + R] + beta * ldown[...]
         ldown[...] = ld
@@ -374,7 +378,7 @@
         scb[place] = share
         @pl.when(it < ITERS - 1)
         def _():
-            for way, far, last, name in ((1, 3, 2, "r_a3p"), (-1, 3, 2, "r_a3m"), (1, 6, 2, "r_a6p"), (-1, 6, 1, "r_a6m")):
+            for way, far, last, name in ((1, 2, 2, "r_a2p"), (-1, 2, 2, "r_a2m"), (1, 5, 3, "r_a5p"), (-1, 5, 2, "r_a5m")):
                 got(img.at[c, 0], name)
                 held = img.at[c, ring(-far * way)]
                 for e in range(last, 0, -1):
@@ -391,9 +395,12 @@
 
         @pl.when(it < ITERS - 1)
         def _():
-            got(img.at[c, pl.ds(0, 4)], "r_ad")
-            got(img.at[c, pl.ds(0, 7)], "r_ax")
-            put(img.at[c], img.at[c], "s_pag", "r_pag", partner)
+            got(img.at[c, pl.ds(0, 2)], "r_ad")
+            for e in (0, 1, -1, 2, -2, 5, -5):
+                put(img.at[c, ring(e)], img.at[c, ring(e)], "s_pag", "r_pag", partner)
+            got(img.at[c, pl.ds(0, 9)], "r_ax")
+            for e in (3, -3, 4, -4, 6, -6, 7, -7, 8):
+                put(img.at[c, ring(e)], img.at[c, ring(e)], "s_pag", "r_pag", partner)
             sent(img.at[c, pl.ds(0, 15)], "s_ag")
 
         sent(xyr.at[pl.ds(0, XY - 1)], "s_xy")
@@ -424,11 +431,11 @@
     hbm = pl.BlockSpec(memory_space=pltpu.HBM)
     scratch = [
         ((rows, cols), F32),
-        ((rows, cols), BF16), ((rows, cols), BF16), ((2, cols, cols), BF16), ((2, cols, cols), BF16),
-        ((640, 256), BF16), ((640, 256), BF16),
+        ((rows, 2 * cols), BF16), ((2, cols, 2 * cols), BF16),
+        ((2 * cols, 256), BF16), ((2 * cols, 256), BF16),
         ((2, *chunks), F32), (chunks, F32),
-        ((2, R, 128), F32), ((1, R, 128), F32), ((2, R, 128), F32), ((2, R, 128), F32),
-        ((4, R, 128), F32), ((4, R, 128), F32),
+        ((3, R, 128), F32), ((2, R, 128), F32), ((2, R, 128), F32), ((2, R, 128), F32),
+        ((2, R, 128), F32), ((4, R, 128), F32),
         ((2, *chunks), F32), (chunks, F32), (chunks, F32),
         ((2 * HALO + XY + 1, R, 128), F32), (chunks, F32),
         ((R, 128), F32), ((R, 128), F32), ((R, 128), F32),

time: 139 us -> 137 us (0.986)
  Pallas kernels: 137 us -> 135 us
    pallas_call x1, Pallas kernels: 137 us -> 135 us  [shards(): pl.pallas_call(kernel, out_shape=jax.ShapeDtypeStruct(chunks, F32), in_sp...]
where the time goes in v4:
time: 137 us
  Pallas kernels  135 us (99%)
  local copies, waits for them, and re-layouts  1.72 us (1%)
    pallas_call x1, Pallas kernels, shards(): pl.pallas_call(kernel, out_shape=jax.ShapeDtypeStruct(chunks, F32), in_sp...  135 us

profile of v4, /device:TPU:1, one launch (start us, length us, event | category | flops | bytes accessed | tf_op | source)
XLA Modules:
  0.0 136.8 jit_solution(15189180645705416177)
XLA Ops:
  0.0 135.1 %shard_map.46 = f32[16,40,128]{2,1,0:T(8,128)} custom-call(f32[1280,640]{1,0:T(8,128)} %green.1, f32[2,16,40,128]{3,2,1,0:T(8,128)} %bitcast.4, s32[3,640]{1,0:T(4,128)} %neighbours.1, f32[1,128]{1,0:T(1,128)} %bitcast.5), custom_call_target="tpu_custom_call" | custom-call | tf_op jit(solution)/shard_map/pallas_call | solution.py:446
  135.1 1.7 %copy.6 = f32[640,128]{1,0:T(8,128)} copy(f32[640,128]{1,0:T(8,128)} %bitcast.3) | data formatting | bytes 655360
